TPU v7x, 32 devices: a whole 2x2x4 slice. The times are simulated.
32 devices in a mesh: elem: 8 (over z, core), lev: 4 (over y, x).
Axes of the slice: x: 2, y: 2, z: 4, core: 2. Of those that a mesh axis runs over, the one named last changes fastest.
Arguments:
- tracers: float32 [512, 16, 640], P('elem', 'lev'), may hold values from 0.1 to 120, as said below
- ref_index: int32 [512, 16], P('elem'), may hold values from 0 to 63
- requests: int32 [8, 2, 16], P('elem'), may hold values from -1 to 63, as said below
- source: int32 [512], P('elem'), may hold values from 0 to 95, as said below
- target_mean: float32 [40], replicated, may hold values from 0.5 to 5
Outputs:
- transported: float32 [512, 16, 640], P('elem', 'lev')
Inputs may be any that keep to these rules, and one draw needn't show every extreme that they name: Row 0 of requests[d] holds distinct element indices of block d - 1 (wrapping), row 1 of block d + 1; the valid entries come first and the rest are -1; every row holds 1 to 16 valid entries and some row holds exactly 16. `source`: every slot names an own element (below 64) or a valid entry of the block's requests: 64 + k for row 0, 80 + k for row 1. `tracers`: all entries are positive.
All inputs are finite; a program needn't handle non-finite values.
Results may differ from a plain program's by a relative error of at most 0.0003.
Values sent between devices are 32-bit elements; how exact they have to be, the bound alone decides.
A program may use at most 64 MiB of HBM per device.

v0:
```python
import math
import jax
import jax.numpy as jnp
from jax import lax
from jax.sharding import PartitionSpec as P

NPTS = 16
REFS = 64


def with_halo(cells, sides, width):
    for axis, dim in sides:
        count = lax.axis_size(axis)
        head = lax.slice_in_dim(cells, 0, width, axis=dim)
        tail = lax.slice_in_dim(cells, cells.shape[dim] - width, cells.shape[dim], axis=dim)
        cells = jnp.concatenate(
            [
                lax.ppermute(tail, axis, [(i, (i + 1) % count) for i in range(count)]),
                cells,
                lax.ppermute(head, axis, [((i + 1) % count, i) for i in range(count)]),
            ],
            axis=dim,
        )
    return cells


def lagrange_table():
    side = math.isqrt(REFS)
    gll_nodes = [-1.0, -math.sqrt(0.2), math.sqrt(0.2), 1.0]
    points = -1.0 + 2.0 * jnp.arange(side, dtype=jnp.float32) / (side - 1)
    columns = []
    for which in range(4):
        basis = jnp.ones((side,), jnp.float32)
        for other in range(4):
            if other != which:
                basis = basis * (points - gll_nodes[other]) / (gll_nodes[which] - gll_nodes[other])
        columns.append(basis)
    one_dim = jnp.stack(columns, axis=1)
    return (one_dim[:, None, :, None] * one_dim[None, :, None, :]).reshape(side * side, 16)


def quadrature():
    edge = jnp.array([1.0 / 6.0, 5.0 / 6.0, 5.0 / 6.0, 1.0 / 6.0], jnp.float32)
    return (edge[:, None] * edge[None, :]).reshape(16)


def interpolate(source_rows, ref_index):
    elem_count, levels, width = source_rows.shape
    onehot = (ref_index[:, :, None] == jnp.arange(REFS, dtype=jnp.int32)[None, None, :]).astype(
        jnp.float32
    )
    matrix = jnp.einsum("epr,rn->epn", onehot, lagrange_table(), precision=lax.Precision.HIGHEST)
    values = source_rows.reshape(elem_count, levels * (width // 16), 16)
    result = jnp.einsum("epn,ecn->ecp", matrix, values, precision=lax.Precision.HIGHEST)
    lowest = jnp.min(values, axis=2, keepdims=True)
    highest = jnp.max(values, axis=2, keepdims=True)
    result = jnp.minimum(jnp.maximum(result, lowest), highest)
    return result.reshape(elem_count, levels, width)


def per_device(tracers, ref_index, requests, source, target_mean):
    elem_count, levels, width = tracers.shape
    beside_all = with_halo(tracers, (("elem", 0),), elem_count)
    own_pos = jnp.arange(elem_count, 2 * elem_count, dtype=jnp.int32)
    left_pos = jnp.maximum(requests[0, 0], 0)
    right_pos = 2 * elem_count + jnp.maximum(requests[0, 1], 0)
    slot_pos = jnp.concatenate([own_pos, left_pos, right_pos])
    source_rows = beside_all[slot_pos[source]]
    clipped = interpolate(source_rows, ref_index)
    tracer_count = width // NPTS
    shaped = clipped.reshape(elem_count, levels, tracer_count, NPTS)
    local_mass = jnp.einsum("eltn,n->t", shaped, quadrature(), precision=lax.Precision.HIGHEST)
    column_mass = lax.psum(local_mass, "lev")
    global_mass = lax.psum(column_mass, "elem")
    whole_weight = 4.0 * elem_count * lax.axis_size("elem") * levels * lax.axis_size("lev")
    factor = target_mean * whole_weight / global_mass
    return (shaped * factor[None, None, :, None]).reshape(elem_count, levels, width)


def solution(mesh):
    placed = (P("elem", "lev", None), P("elem", None), P("elem", None, None), P("elem"), P())
    return jax.shard_map(
        per_device, mesh=mesh, in_specs=placed, out_specs=P("elem", "lev", None), check_vma=False
    )
```

profile of v0, /device:TPU:0, one launch (start us, length us, event | category | flops | bytes accessed | tf_op | source)
XLA Modules:
  0.0 54.3 jit_solution(1006085163537011619)
XLA Ops:
  0.0 4.5 %collective-permute-start.1 = (f32[64,4,640]{2,1,0:T(4,128)}, f32[64,4,640]{2,1,0:T(4,128)S(1)}, u32[]{:S(2)}, u32[]{:S(2)}) collective-permute-start(f32[64,4,640]{2,1,0:T(4,128)} %param.6), channel_id=1, source_target_pairs={{4,0},{8,4},{12,8},{16,12},{20,16},{24,20},{28,24},{0,28},{5,1},{9... | collective-permute-start | bytes 1966088 | tf_op jit(solution)/shard_map/ppermute | solution.py:20
  4.5 0.0 collective-permute-start
  4.6 0.8 %maximum_bitcast_fusion = (s32[16]{0:T(128)S(1)}, s32[16]{0:T(128)S(1)}) fusion(s32[1,2,16]{2,1,0:T(2,128)} %param.8), kind=kLoop, calls=%fused_computation.29 | loop fusion | flops 48 | bytes 256 | tf_op jit(solution)/shard_map/max | solution.py:65
  5.3 0.1 broadcast_multiply_fusion
  5.4 0.1 reshape.146
  5.5 1.5 %fusion.1 = f32[64,16,16]{0,2,1:T(8,128)S(1)} fusion(f32[64,16,1]{0,1,2:T(8,128)S(1)} %reshape.146, s32[64,16]{0,1:T(8,128)} %param.7), kind=kOutput, calls=%fused_computation.8 | convolution fusion | flops 12648448 | bytes 73728 | tf_op jit(solution)/shard_map/epr,rn->epn/dot_general | solution.py:52
  7.0 1.0 %copy.23 = f32[64,16,16]{2,1,0:T(8,128)} copy(f32[64,16,16]{0,2,1:T(8,128)S(1)} %fusion.1) | data formatting | bytes 131072 | tf_op jit(solution)/shard_map/epr,rn->epn/dot_general | solution.py:52
  8.0 0.8 %broadcast_multiply_fusion.1 = f32[4,4]{1,0:T(4,128)S(1)} fusion(f32[4]{0:T(128)} %constant.76.clone), kind=kLoop, calls=%fused_computation.16 | loop fusion | flops 16 | bytes 80 | tf_op jit(solution)/shard_map/mul | solution.py:44
  8.8 0.1 reshape.147
  8.9 0.1 pad_add_fusion
  9.0 0.7 %compare_select_fusion.1 = s32[64]{0:T(128)S(1)} fusion(s32[64]{0:T(128)} %param.9), kind=kLoop, calls=%fused_computation.14 | loop fusion | flops 192 | bytes 512 | tf_op jit(solution)/shard_map/select_n | solution.py:68
  9.6 0.8 %gather_fusion = s32[64]{0:T(128)S(1)} fusion(s32[96]{0:T(128)S(1)} %pad_add_fusion, s32[1024]{0:T(1024)S(1)} %pad_clamp_fusion.1), kind=kCustom, calls=%fused_computation | custom fusion | bytes 768 | tf_op jit(solution)/shard_map/gather | solution.py:68
  10.4 7.6 %collective-permute-done.1 = f32[64,4,640]{2,1,0:T(4,128)S(1)} collective-permute-done((f32[64,4,640]{2,1,0:T(4,128)}, f32[64,4,640]{2,1,0:T(4,128)S(1)}, u32[]{:S(2)}, u32[]{:S(2)}) %collective-permute-start.1) | collective-permute-done | bytes 655392 | tf_op jit(solution)/shard_map/ppermute | solution.py:20
  18.0 3.0 %collective-permute-done = f32[64,4,640]{2,1,0:T(4,128)} collective-permute-done((f32[64,4,640]{2,1,0:T(4,128)}, f32[64,4,640]{2,1,0:T(4,128)}, u32[]{:S(2)}, u32[]{:S(2)}) %collective-permute-start) | collective-permute-done | bytes 655392 | tf_op jit(solution)/shard_map/ppermute | solution.py:18
  21.1 1.5 %pad_maximum_fusion = f32[192,4,640]{2,1,0:T(4,128)S(1)} fusion(f32[64,4,640]{2,1,0:T(4,128)S(1)} %collective-permute-done.1, f32[64,4,640]{2,1,0:T(4,128)S(1)} %copy-done, f32[64,4,640]{2,1,0:T(4,128)} %collective-permute-done), kind=kLoop, calls=%fused_computation.2 | loop fusion | flops 983040 | bytes 3932160 | tf_op jit(solution)/shard_map/concatenate | solution.py:16
  22.6 1.0 %gather_fusion.1 = f32[64,4,640]{2,1,0:T(4,128)S(1)} fusion(f32[192,4,640]{2,1,0:T(4,128)S(1)} %pad_maximum_fusion, s32[1024]{0:T(1024)S(1)} %pad_clamp_fusion), kind=kCustom, calls=%fused_computation.1 | custom fusion | bytes 1310976 | tf_op jit(solution)/shard_map/gather | solution.py:68
  23.5 0.4 copy.21
  24.0 0.5 fusion.7
  24.5 1.1 %copy.22 = f32[64,160,16]{1,2,0:T(8,128)S(1)} copy(f32[64,160,16]{0,2,1:T(8,128)S(1)} %bitcast.26) | data formatting | bytes 1310720 | tf_op jit(solution)/shard_map/reshape | solution.py:53
  25.6 0.0 copy-start.1
  25.6 0.1 copy.25
  25.7 0.1 copy.24
  25.8 2.1 %fusion.8 = (f32[160,16]{0,1:T(8,128)S(1)}, f32[64,160,16]{1,2,0:T(8,128)S(1)}) fusion(f32[64,160]{1,0:T(8,128)S(1)} %copy.25, f32[64,160]{1,0:T(8,128)S(1)} %copy.24, f32[64,160,16]{1,2,0:T(8,128)S(1)} %copy.22, f32[64,16,16]{2,1,0:T(8,128)} %copy.23), kind=kOutput, calls=%fused_computation.32 | convolution fusion | flops 31946240 | bytes 1468416 | tf_op jit(solution)/shard_map/epn,ecn->ecp/dot_general | solution.py:54
  28.0 0.1 reduce_sum.14
  28.1 0.1 convolution_bitcast_fusion
  28.2 9.9 %psum.14 = f32[40]{0:T(128)S(1)} all-reduce(f32[40]{0:T(128)S(1)} %convolution_bitcast_fusion), channel_id=1, replica_groups=mesh['elem'=8,'lev'=4] {'lev'}, use_global_device_ids=true, to_apply=%region_4.0 | all-reduce | flops 40 | bytes 320 | tf_op jit(solution)/shard_map/psum | solution.py:73
  38.1 13.6 %psum.15 = f32[40]{0:T(128)S(1)} all-reduce(f32[40]{0:T(128)S(1)} %psum.14), channel_id=1, replica_groups=mesh['elem'=8,'lev'=4] {'elem'}, use_global_device_ids=true, to_apply=%region_5.6 | all-reduce | flops 40 | bytes 320 | tf_op jit(solution)/shard_map/psum | solution.py:74
  51.7 0.1 mul.156
  51.8 0.1 mul.157
  51.8 1.1 %copy.26 = f32[64,160,16]{0,2,1:T(8,128)S(1)} copy(f32[64,160,16]{1,2,0:T(8,128)S(1)} %get-tuple-element.10) | data formatting | bytes 1310720 | tf_op jit(solution)/shard_map/min | solution.py:57
  52.9 0.2 bitcast_multiply_fusion
  53.1 1.2 %copy.27 = f32[64,4,640]{2,1,0:T(4,128)} copy(f32[64,4,640]{0,2,1:T(8,128)S(1)} %bitcast_multiply_fusion) | data formatting | bytes 1310720 | tf_op jit(solution)/shard_map/mul | solution.py:77
  (12 shorter events, 0.1 us)
Async XLA Ops:
  0.0 21.1 %copy-start = (f32[64,4,640]{2,1,0:T(4,128)S(1)}, f32[64,4,640]{2,1,0:T(4,128)}, u32[]{:S(2)}) copy-start(f32[64,4,640]{2,1,0:T(4,128)} %param.6) | copy-start | bytes 1966084
  0.0 18.0 %collective-permute-start.1 = (f32[64,4,640]{2,1,0:T(4,128)}, f32[64,4,640]{2,1,0:T(4,128)S(1)}, u32[]{:S(2)}, u32[]{:S(2)}) collective-permute-start(f32[64,4,640]{2,1,0:T(4,128)} %param.6), channel_id=1, source_target_pairs={{4,0},{8,4},{12,8},{16,12},{20,16},{24,20},{28,24},{0,28},{5,1},{9... | collective-permute-start | bytes 1966088 | tf_op jit(solution)/shard_map/ppermute | solution.py:20
  4.5 16.5 %collective-permute-start = (f32[64,4,640]{2,1,0:T(4,128)}, f32[64,4,640]{2,1,0:T(4,128)}, u32[]{:S(2)}, u32[]{:S(2)}) collective-permute-start(f32[64,4,640]{2,1,0:T(4,128)} %param.6), channel_id=1, source_target_pairs={{0,4},{4,8},{8,12},{12,16},{16,20},{20,24},{24,28},{28,0},{1,5},{5... | collective-permute-start | bytes 1966088 | tf_op jit(solution)/shard_map/ppermute | solution.py:18
  25.6 26.1 %copy-start.1 = (f32[40]{0:T(128)S(1)}, f32[40]{0:T(128)}, u32[]{:S(2)}) copy-start(f32[40]{0:T(128)} %param.10) | copy-start | bytes 484
where the time goes:
time: 54.6 us; the launch traced here: 54.3 us
  blocking collectives  23.5 us (43%)
  waiting for transfers between devices  10.6 us (19%)
  local copies, waits for them, and re-layouts  7.18 us (13%)
  other arithmetic  4.66 us (9%)
  starting transfers between devices  4.52 us (8%)
  matrix products  3.75 us (7%)
    psum x1, blocking collectives, per_device(): global_mass = lax.psum(column_mass, 'elem')  13.6 us
    psum x1, blocking collectives, per_device(): column_mass = lax.psum(local_mass, 'lev')  9.89 us
    ppermute x1, waiting for transfers between devices, with_halo(): lax.ppermute(head, axis, [((i + 1) % count, i) for i in range(count)])  7.59 us
    ppermute x1, starting transfers between devices, with_halo(): lax.ppermute(head, axis, [((i + 1) % count, i) for i in range(count)])  4.52 us
    ppermute x1, waiting for transfers between devices, with_halo(): lax.ppermute(tail, axis, [(i, (i + 1) % count) for i in range(count)])  3.03 us
    gather x3, local copies, waits for them, and re-layouts, per_device(): source_rows = beside_all[slot_pos[source]]  2.17 us
    dot_general x1, matrix products, interpolate(): jnp.einsum('epn,ecn->ecp', matrix, values, precision=lax.Precision.HIGHEST)  2.15 us
    concatenate x1, other arithmetic, with_halo(): jnp.concatenate([lax.ppermute(tail, axis, [(i, (i + 1) % count) for i in...  1.51 us
  transfers between devices with their start and end apart: 2, of which 2 were waited for; matrix products, arithmetic and copies ran while one was open for 11% of the time, Pallas kernels for 0%

commit v1 on v0

--- a/solution.py
+++ b/solution.py
@@ -70,7 +70,11 @@
     tracer_count = width // NPTS
     shaped = clipped.reshape(elem_count, levels, tracer_count, NPTS)
     local_mass = jnp.einsum("eltn,n->t", shaped, quadrature(), precision=lax.Precision.HIGHEST)
-    column_mass = lax.psum(local_mass, "lev")
+    column_mass = local_mass
+    for hop in (1, 2):
+        column_mass = column_mass + lax.ppermute(
+            column_mass, "lev", [(dev, dev ^ hop) for dev in range(4)]
+        )
     global_mass = lax.psum(column_mass, "elem")
     whole_weight = 4.0 * elem_count * lax.axis_size("elem") * levels * lax.axis_size("lev")
     factor = target_mean * whole_weight / global_mass

time: 54.6 us -> 50.8 us (0.930)
  blocking collectives: 23.5 us -> 13.6 us
  waiting for transfers between devices: 10.6 us -> 13.7 us
  starting transfers between devices: 4.52 us -> 7.54 us
    psum x1 -> x0, blocking collectives: 9.89 us -> none  [per_device(): column_mass = lax.psum(local_mass, 'lev')]
    ppermute x0 -> x2, waiting for transfers between devices: none -> 3.06 us  [per_device(): lax.ppermute(column_mass, 'lev', [(dev, dev ^ hop) for dev in range(4)])]
    ppermute x0 -> x2, starting transfers between devices: none -> 3.02 us  [per_device(): lax.ppermute(column_mass, 'lev', [(dev, dev ^ hop) for dev in range(4)])]
  transfers between devices with their start and end apart: 2 -> 4, of which waited for: 2 -> 4; matrix products, arithmetic and copies ran while one was open for 11% -> 14% of each run, Pallas kernels for 0% -> 0%
where the time goes in v1:
time: 50.8 us; the launch traced here: 50.5 us
  waiting for transfers between devices  13.7 us (27%)
  blocking collectives  13.6 us (27%)
  starting transfers between devices  7.54 us (15%)
  local copies, waits for them, and re-layouts  7.17 us (14%)
  other arithmetic  4.68 us (9%)
  matrix products  3.75 us (7%)
    psum x1, blocking collectives, per_device(): global_mass = lax.psum(column_mass, 'elem')  13.6 us
    ppermute x1, waiting for transfers between devices, with_halo(): lax.ppermute(head, axis, [((i + 1) % count, i) for i in range(count)])  7.59 us
    ppermute x1, starting transfers between devices, with_halo(): lax.ppermute(head, axis, [((i + 1) % count, i) for i in range(count)])  4.52 us
    ppermute x2, waiting for transfers between devices, per_device(): lax.ppermute(column_mass, 'lev', [(dev, dev ^ hop) for dev in range(4)])  3.06 us
    ppermute x1, waiting for transfers between devices, with_halo(): lax.ppermute(tail, axis, [(i, (i + 1) % count) for i in range(count)])  3.03 us
    ppermute x2, starting transfers between devices, per_device(): lax.ppermute(column_mass, 'lev', [(dev, dev ^ hop) for dev in range(4)])  3.02 us
    gather x3, local copies, waits for them, and re-layouts, per_device(): source_rows = beside_all[slot_pos[source]]  2.17 us
    dot_general x1, matrix products, interpolate(): jnp.einsum('epn,ecn->ecp', matrix, values, precision=lax.Precision.HIGHEST)  2.15 us
  transfers between devices with their start and end apart: 4, of which 4 were waited for; matrix products, arithmetic and copies ran while one was open for 14% of the time, Pallas kernels for 0%

profile of v1, /device:TPU:0, one launch (start us, length us, event | category | flops | bytes accessed | tf_op | source)
XLA Modules:
  0.0 50.5 jit_solution(17054327741406898953)
XLA Ops:
  0.0 4.5 %collective-permute-start.1 = (f32[64,4,640]{2,1,0:T(4,128)}, f32[64,4,640]{2,1,0:T(4,128)S(1)}, u32[]{:S(2)}, u32[]{:S(2)}) collective-permute-start(f32[64,4,640]{2,1,0:T(4,128)} %param.6), channel_id=1, source_target_pairs={{4,0},{8,4},{12,8},{16,12},{20,16},{24,20},{28,24},{0,28},{5,1},{9... | collective-permute-start | bytes 1966088 | tf_op jit(solution)/shard_map/ppermute | solution.py:20
  4.6 0.8 %maximum_bitcast_fusion = (s32[16]{0:T(128)S(1)}, s32[16]{0:T(128)S(1)}) fusion(s32[1,2,16]{2,1,0:T(2,128)} %param.8), kind=kLoop, calls=%fused_computation.29 | loop fusion | flops 48 | bytes 256 | tf_op jit(solution)/shard_map/max | solution.py:65
  5.3 0.1 broadcast_multiply_fusion
  5.4 0.1 reshape.146
  5.5 1.5 %fusion.1 = f32[64,16,16]{0,2,1:T(8,128)S(1)} fusion(f32[64,16,1]{0,1,2:T(8,128)S(1)} %reshape.146, s32[64,16]{0,1:T(8,128)} %param.7), kind=kOutput, calls=%fused_computation.8 | convolution fusion | flops 12648448 | bytes 73728 | tf_op jit(solution)/shard_map/epr,rn->epn/dot_general | solution.py:52
  7.0 1.0 %copy.23 = f32[64,16,16]{2,1,0:T(8,128)} copy(f32[64,16,16]{0,2,1:T(8,128)S(1)} %fusion.1) | data formatting | bytes 131072 | tf_op jit(solution)/shard_map/epr,rn->epn/dot_general | solution.py:52
  8.0 0.8 %broadcast_multiply_fusion.1 = f32[4,4]{1,0:T(4,128)S(1)} fusion(f32[4]{0:T(128)} %constant.76.clone), kind=kLoop, calls=%fused_computation.16 | loop fusion | flops 16 | bytes 80 | tf_op jit(solution)/shard_map/mul | solution.py:44
  8.8 0.1 reshape.147
  8.9 0.1 pad_add_fusion
  9.0 0.7 %compare_select_fusion.1 = s32[64]{0:T(128)S(1)} fusion(s32[64]{0:T(128)} %param.9), kind=kLoop, calls=%fused_computation.14 | loop fusion | flops 192 | bytes 512 | tf_op jit(solution)/shard_map/select_n | solution.py:68
  9.6 0.8 %gather_fusion = s32[64]{0:T(128)S(1)} fusion(s32[96]{0:T(128)S(1)} %pad_add_fusion, s32[1024]{0:T(1024)S(1)} %pad_clamp_fusion.1), kind=kCustom, calls=%fused_computation | custom fusion | bytes 768 | tf_op jit(solution)/shard_map/gather | solution.py:68
  10.4 7.6 %collective-permute-done.1 = f32[64,4,640]{2,1,0:T(4,128)S(1)} collective-permute-done((f32[64,4,640]{2,1,0:T(4,128)}, f32[64,4,640]{2,1,0:T(4,128)S(1)}, u32[]{:S(2)}, u32[]{:S(2)}) %collective-permute-start.1) | collective-permute-done | bytes 655392 | tf_op jit(solution)/shard_map/ppermute | solution.py:20
  18.0 3.0 %collective-permute-done = f32[64,4,640]{2,1,0:T(4,128)} collective-permute-done((f32[64,4,640]{2,1,0:T(4,128)}, f32[64,4,640]{2,1,0:T(4,128)}, u32[]{:S(2)}, u32[]{:S(2)}) %collective-permute-start) | collective-permute-done | bytes 655392 | tf_op jit(solution)/shard_map/ppermute | solution.py:18
  21.1 1.5 %pad_maximum_fusion = f32[192,4,640]{2,1,0:T(4,128)S(1)} fusion(f32[64,4,640]{2,1,0:T(4,128)S(1)} %collective-permute-done.1, f32[64,4,640]{2,1,0:T(4,128)S(1)} %copy-done, f32[64,4,640]{2,1,0:T(4,128)} %collective-permute-done), kind=kLoop, calls=%fused_computation.2 | loop fusion | flops 983040 | bytes 3932160 | tf_op jit(solution)/shard_map/concatenate | solution.py:16
  22.6 1.0 %gather_fusion.1 = f32[64,4,640]{2,1,0:T(4,128)S(1)} fusion(f32[192,4,640]{2,1,0:T(4,128)S(1)} %pad_maximum_fusion, s32[1024]{0:T(1024)S(1)} %pad_clamp_fusion), kind=kCustom, calls=%fused_computation.1 | custom fusion | bytes 1310976 | tf_op jit(solution)/shard_map/gather | solution.py:68
  23.5 0.4 copy.21
  24.0 0.5 %fusion.7 = (f32[64,160]{0,1:T(8,128)S(1)}, f32[64,160]{0,1:T(8,128)S(1)}) fusion(f32[64,160,16]{0,2,1:T(8,128)S(1)} %bitcast.25), kind=kLoop, calls=%fused_computation.31 | loop fusion | flops 307200 | bytes 737280 | tf_op jit(solution)/shard_map/reduce_min | solution.py:55
  24.5 1.1 %copy.22 = f32[64,160,16]{1,2,0:T(8,128)S(1)} copy(f32[64,160,16]{0,2,1:T(8,128)S(1)} %bitcast.26) | data formatting | bytes 1310720 | tf_op jit(solution)/shard_map/reshape | solution.py:53
  25.6 0.1 copy.25
  25.7 0.1 copy.24
  25.8 2.1 %fusion.8 = (f32[160,16]{0,1:T(8,128)S(1)}, f32[64,160,16]{1,2,0:T(8,128)S(1)}) fusion(f32[64,160]{1,0:T(8,128)S(1)} %copy.25, f32[64,160]{1,0:T(8,128)S(1)} %copy.24, f32[64,160,16]{1,2,0:T(8,128)S(1)} %copy.22, f32[64,16,16]{2,1,0:T(8,128)} %copy.23), kind=kOutput, calls=%fused_computation.32 | convolution fusion | flops 31946240 | bytes 1468416 | tf_op jit(solution)/shard_map/epn,ecn->ecp/dot_general | solution.py:54
  28.0 0.1 reduce_sum.14
  28.1 0.1 convolution_bitcast_fusion
  28.2 1.5 %collective-permute-start.2 = (f32[40]{0:T(128)S(1)}, f32[40]{0:T(128)S(1)}, u32[]{:S(2)}, u32[]{:S(2)}) collective-permute-start(f32[40]{0:T(128)S(1)} %convolution_bitcast_fusion), channel_id=1, source_target_pairs={{0,1},{1,0},{2,3},{3,2},{4,5},{5,4},{6,7},{7,6},{8,9},{9,8},{10,11... | collective-permute-start | bytes 488 | tf_op jit(solution)/shard_map/ppermute | solution.py:75
  29.7 2.1 %collective-permute-done.2 = f32[40]{0:T(128)S(1)} collective-permute-done((f32[40]{0:T(128)S(1)}, f32[40]{0:T(128)S(1)}, u32[]{:S(2)}, u32[]{:S(2)}) %collective-permute-start.2) | collective-permute-done | bytes 192 | tf_op jit(solution)/shard_map/ppermute | solution.py:75
  31.8 1.5 %collective-permute-start.3 = (f32[40]{0:T(128)S(1)}, f32[40]{0:T(128)S(1)}, u32[]{:S(2)}, u32[]{:S(2)}) collective-permute-start(f32[40]{0:T(128)S(1)} %add.116), channel_id=1, source_target_pairs={{0,2},{1,3},{2,0},{3,1},{4,6},{5,7},{6,4},{7,5},{8,10},{9,11},{10,... | collective-permute-start | bytes 488 | tf_op jit(solution)/shard_map/ppermute | solution.py:75
  33.3 1.1 %copy.26 = f32[64,160,16]{0,2,1:T(8,128)S(1)} copy(f32[64,160,16]{1,2,0:T(8,128)S(1)} %get-tuple-element.10) | data formatting | bytes 1310720 | tf_op jit(solution)/shard_map/min | solution.py:57
  34.4 1.0 %collective-permute-done.3 = f32[40]{0:T(128)S(1)} collective-permute-done((f32[40]{0:T(128)S(1)}, f32[40]{0:T(128)S(1)}, u32[]{:S(2)}, u32[]{:S(2)}) %collective-permute-start.3) | collective-permute-done | bytes 192 | tf_op jit(solution)/shard_map/ppermute | solution.py:75
  35.4 13.6 %psum.7 = f32[40]{0:T(128)S(1)} all-reduce(f32[40]{0:T(128)S(1)} %add.117), channel_id=1, replica_groups=mesh['elem'=8,'lev'=4] {'elem'}, use_global_device_ids=true, to_apply=%region_4.5 | all-reduce | flops 40 | bytes 320 | tf_op jit(solution)/shard_map/psum | solution.py:78
  49.0 0.1 mul.157
  49.1 0.2 bitcast_multiply_fusion
  49.3 1.2 %copy.27 = f32[64,4,640]{2,1,0:T(4,128)} copy(f32[64,4,640]{0,2,1:T(8,128)S(1)} %bitcast_multiply_fusion) | data formatting | bytes 1310720 | tf_op jit(solution)/shard_map/mul | solution.py:81
  (17 shorter events, 0.2 us)
Async XLA Ops:
  0.0 21.1 %copy-start = (f32[64,4,640]{2,1,0:T(4,128)S(1)}, f32[64,4,640]{2,1,0:T(4,128)}, u32[]{:S(2)}) copy-start(f32[64,4,640]{2,1,0:T(4,128)} %param.6) | copy-start | bytes 1966084
  0.0 18.0 %collective-permute-start.1 = (f32[64,4,640]{2,1,0:T(4,128)}, f32[64,4,640]{2,1,0:T(4,128)S(1)}, u32[]{:S(2)}, u32[]{:S(2)}) collective-permute-start(f32[64,4,640]{2,1,0:T(4,128)} %param.6), channel_id=1, source_target_pairs={{4,0},{8,4},{12,8},{16,12},{20,16},{24,20},{28,24},{0,28},{5,1},{9... | collective-permute-start | bytes 1966088 | tf_op jit(solution)/shard_map/ppermute | solution.py:20
  4.5 16.5 %collective-permute-start = (f32[64,4,640]{2,1,0:T(4,128)}, f32[64,4,640]{2,1,0:T(4,128)}, u32[]{:S(2)}, u32[]{:S(2)}) collective-permute-start(f32[64,4,640]{2,1,0:T(4,128)} %param.6), channel_id=1, source_target_pairs={{0,4},{4,8},{8,12},{12,16},{16,20},{20,24},{24,28},{28,0},{1,5},{5... | collective-permute-start | bytes 1966088 | tf_op jit(solution)/shard_map/ppermute | solution.py:18
  25.8 23.1 %copy-start.1 = (f32[40]{0:T(128)S(1)}, f32[40]{0:T(128)}, u32[]{:S(2)}) copy-start(f32[40]{0:T(128)} %param.10) | copy-start | bytes 484
  28.2 3.6 %collective-permute-start.2 = (f32[40]{0:T(128)S(1)}, f32[40]{0:T(128)S(1)}, u32[]{:S(2)}, u32[]{:S(2)}) collective-permute-start(f32[40]{0:T(128)S(1)} %convolution_bitcast_fusion), channel_id=1, source_target_pairs={{0,1},{1,0},{2,3},{3,2},{4,5},{5,4},{6,7},{7,6},{8,9},{9,8},{10,11... | collective-permute-start | bytes 488 | tf_op jit(solution)/shard_map/ppermute | solution.py:75
  31.8 3.6 %collective-permute-start.3 = (f32[40]{0:T(128)S(1)}, f32[40]{0:T(128)S(1)}, u32[]{:S(2)}, u32[]{:S(2)}) collective-permute-start(f32[40]{0:T(128)S(1)} %add.116), channel_id=1, source_target_pairs={{0,2},{1,3},{2,0},{3,1},{4,6},{5,7},{6,4},{7,5},{8,10},{9,11},{10,... | collective-permute-start | bytes 488 | tf_op jit(solution)/shard_map/ppermute | solution.py:75
